TPU v7x, 512 devices: a whole 4x4x16 slice. The times are simulated.
512 devices in a mesh: layer: 8 (over y, z_hi), row: 4 (over x), col: 16 (over z_lo, core).
Axes of the slice: x: 4, y: 4, z: 16 (z_hi: 2, z_lo: 8; z = z_hi * 8 + z_lo), core: 2. Of those that a mesh axis runs over, the one named last changes fastest.
Arguments:
- subtree_terms: float32 [8, 4096, 4096], P('layer', 'row', 'col')
- order: int32 [2], replicated, may hold values from 0 to 1, each once
Outputs:
- factored: float32 [4096, 4096], P('row', 'col')
Inputs may be any that keep to these rules, and one draw needn't show every extreme that they name: `order`: each of 0 .. 1 appears once.
All inputs are finite; a program needn't handle non-finite values.
Results may differ from a plain program's by a relative error of at most 0.0003.
Values sent between devices are 32-bit elements; how exact they have to be, the bound alone decides.
A program may use at most 64 MiB of HBM per device.

v0:
```python
import jax
import jax.numpy as jnp
from jax import lax
from jax.sharding import PartitionSpec as P

NB = 128
NP = 2


def split_up(array, dim, count):
    dims = array.shape
    parts = array.reshape(*dims[:dim], count, dims[dim] // count, *dims[dim + 1 :])
    return jnp.moveaxis(parts, dim, 0)


def sum_at_owner(array, axis, dim):
    count = lax.axis_size(axis)
    parts = lax.all_to_all(split_up(array, dim, count), axis, 0, 0, tiled=True)
    return jnp.sum(parts, axis=0)


def from_root(array, axis, root):
    return lax.dynamic_index_in_dim(lax.all_gather(array, axis), root, 0, keepdims=False)


def joined_along(parts, dim):
    parts = jnp.moveaxis(parts, 0, dim)
    dims = parts.shape
    return parts.reshape(*dims[:dim], dims[dim] * dims[dim + 1], *dims[dim + 2 :])


def copy_for_each(array, axis):
    count = lax.axis_size(axis)
    return lax.all_to_all(
        jnp.broadcast_to(array[None], (count, *array.shape)), axis, 0, 0, tiled=True
    )


def gather_directly(array, axis, dim):
    return joined_along(copy_for_each(array, axis), dim)


def invert_block(block):
    size = block.shape[0]
    ident = jnp.eye(size, dtype=jnp.float32)
    index_line = jnp.arange(size)

    def sweep(step, carry):
        mat, inv = carry
        unit = (index_line == step).astype(jnp.float32)
        mat_row = lax.dynamic_index_in_dim(mat, step, 0, keepdims=False)
        inv_row = lax.dynamic_index_in_dim(inv, step, 0, keepdims=False)
        pivot = jnp.sum(mat_row * unit)
        mat_row = mat_row / pivot
        inv_row = inv_row / pivot
        column = jnp.sum(mat * unit[None, :], axis=1) * (1.0 - unit)
        mat = mat - column[:, None] * mat_row[None, :]
        inv = inv - column[:, None] * inv_row[None, :]
        keep = (1.0 - unit)[:, None]
        mat = mat * keep + unit[:, None] * mat_row[None, :]
        inv = inv * keep + unit[:, None] * inv_row[None, :]
        return (mat, inv)

    mat, inv = lax.fori_loop(0, size, sweep, (block, ident))
    return inv


def panel_rank(panel, order):
    hits = panel[:, None] == order[None, :]
    picked = jnp.sum(hits * jnp.arange(NP)[None, :], axis=1)
    return jnp.where(jnp.any(hits, axis=1), picked, NP)


def body(subtree_terms, order):
    front = sum_at_owner(subtree_terms[0], "layer", 0)
    row_start = lax.axis_index("layer") * front.shape[0]
    nrows = lax.axis_size("row")
    ncols = lax.axis_size("col")
    my_row = lax.axis_index("row")
    my_col = lax.axis_index("col")
    local_rows = front.shape[0]
    local_cols = front.shape[1]
    row_q = jnp.arange(local_rows) + row_start
    col_q = jnp.arange(local_cols)
    rank_rows = panel_rank(row_q // NB * nrows + my_row, order)
    rank_cols = panel_rank(col_q // NB * ncols + my_col, order)
    hp = lax.Precision.HIGHEST

    def step(k, front):
        p = order[k]
        row_root = p % nrows
        row_tile = p // nrows
        col_root = p % ncols
        col_start = p // ncols * NB
        row_off = jnp.clip(row_tile * NB - row_start, 0, local_rows - NB)
        rows_block = front
        owner = row_tile * NB // local_rows * nrows + row_root
        rows_block = from_root(rows_block, ("layer", "row"), owner)
        cols_block = lax.dynamic_slice_in_dim(front, col_start, NB, 1)
        diag_block = lax.dynamic_slice_in_dim(rows_block, col_start, NB, 1)
        cols_block, diag_block = (
            from_root(cols_block, "col", col_root),
            from_root(diag_block, "col", col_root),
        )
        inverse = invert_block(diag_block)
        alive_rows = (rank_rows > k).astype(jnp.float32)
        alive_cols = (rank_cols > k).astype(jnp.float32)
        right = jnp.dot(inverse, rows_block * alive_cols[None, :], precision=hp)
        front = front - jnp.dot(cols_block * alive_rows[:, None], right, precision=hp)
        lower = jnp.dot(cols_block, inverse, precision=hp)
        current = lax.dynamic_slice_in_dim(front, col_start, NB, 1)
        writes = jnp.logical_and(alive_rows[:, None] > 0.5, my_col == col_root)
        fresh = jnp.where(writes, lower, current)
        return lax.dynamic_update_slice_in_dim(front, fresh, col_start, 1)

    front = lax.fori_loop(0, NP, step, front)
    front = gather_directly(front, "layer", 0)
    return front


def solution(mesh):
    in_specs = (P("layer", "row", "col"), P())
    out_specs = P("row", "col")
    return jax.shard_map(body, mesh=mesh, in_specs=in_specs, out_specs=out_specs, check_vma=False)
```

profile of v0, /device:TPU:1, one launch (start us, length us, event | category | flops | bytes accessed | tf_op | source)
XLA Modules:
  0.0 1201.3 jit_solution(14813680569260682492)
XLA Ops:
  6.5 18.3 %all-to-all-start = ((f32[8,128,256]{2,1,0:T(8,128)}), f32[8,128,256]{2,1,0:T(8,128)S(1)}, u32[]{:S(2)}, u32[]{:S(2)}) async-start(f32[8,128,256]{2,1,0:T(8,128)} %bitcast.51), calls=%async_computation | async-start | bytes 2097152 | tf_op jit(solution)/shard_map/all_to_all | solution.py:18
  27.8 25.8 %all-to-all-done = f32[8,128,256]{2,1,0:T(8,128)S(1)} async-done(((f32[8,128,256]{2,1,0:T(8,128)}), f32[8,128,256]{2,1,0:T(8,128)S(1)}, u32[]{:S(2)}, u32[]{:S(2)}) %all-to-all-start) | async-done | bytes 1048608 | tf_op jit(solution)/shard_map/all_to_all | solution.py:18
  54.3 1093.3 %while.57 = (s32[]{:T(128)}, f32[128,256]{1,0:T(8,128)}, s32[2]{0:T(128)}, s32[128]{0:T(128)S(1)}, s32[256]{0:T(256)S(1)}, /*index=5*/s32[]{:T(128)}, s32[]{:T(1...) while((s32[]{:T(128)}, f32[128,256]{1,0:T(8,128)}, ...), condition=%wide.region_10.11_spmd, body=%wide.region_5.10_spmd.sunk | while | flops 126159424 | bytes 21511044 | solution.py:116
  55.0 1.3 dynamic_slice.134
  58.8 178.9 %all-gather.10.cloned.1.call-done = f32[4096,256]{1,0:T(8,128)} async-done(((f32[128,256]{1,0:T(8,128)}), f32[4096,256]{1,0:T(8,128)}) %all-gather.10.cloned.1.call-update) | async-done | bytes 4194320 | tf_op jit(solution)/shard_map/while/body/eval_jaxpr/all_gather | solution.py:23
  237.7 1.6 constant_dynamic-slice_fusion.6
  239.4 1.5 constant_dynamic-slice_fusion.7
  241.0 101.3 %all-gather.12.cloned.1.call-done = f32[16,128,128]{2,1,0:T(8,128)} async-done(((f32[1,128,128]{2,1,0:T(8,128)}), f32[16,128,128]{2,1,0:T(8,128)}) %all-gather.12.cloned.1.call-update) | async-done | bytes 1048592 | tf_op jit(solution)/shard_map/while/body/eval_jaxpr/all_gather | solution.py:23
  343.1 263.3 %while.58 = (s32[]{:T(128)}, f32[128,128]{1,0:T(8,128)S(1)}, f32[128,128]{1,0:T(8,128)S(1)}, s32[]{:T(128)}) while((s32[]{:T(128)}, f32[128,128]{1,0:T(8,128)S(1)}, f32[128,128]{1,0:T(8,128)S(1)}, s32[]{:T(128)}) %tuple.79), condition=%wide.region_9.9_spmd.clone, body=%wide.region_6.8_spmd.clone.sunk | while | flops 198145 | bytes 336977 | solution.py:64
  606.4 1.2 fusion.40
  607.6 1.9 convolution_subtract_fusion.2
  609.5 1.7 fusion.41
  611.8 1.3 dynamic_slice.134
  615.6 158.6 %all-gather.10.cloned.1.call-done = f32[4096,256]{1,0:T(8,128)} async-done(((f32[128,256]{1,0:T(8,128)}), f32[4096,256]{1,0:T(8,128)}) %all-gather.10.cloned.1.call-update) | async-done | bytes 4194320 | tf_op jit(solution)/shard_map/while/body/eval_jaxpr/all_gather | solution.py:23
  774.2 1.6 constant_dynamic-slice_fusion.6
  775.9 1.5 constant_dynamic-slice_fusion.7
  777.5 101.2 %all-gather.12.cloned.1.call-done = f32[16,128,128]{2,1,0:T(8,128)} async-done(((f32[1,128,128]{2,1,0:T(8,128)}), f32[16,128,128]{2,1,0:T(8,128)}) %all-gather.12.cloned.1.call-update) | async-done | bytes 1048592 | tf_op jit(solution)/shard_map/while/body/eval_jaxpr/all_gather | solution.py:23
  879.5 263.3 %while.58 = (s32[]{:T(128)}, f32[128,128]{1,0:T(8,128)S(1)}, f32[128,128]{1,0:T(8,128)S(1)}, s32[]{:T(128)}) while((s32[]{:T(128)}, f32[128,128]{1,0:T(8,128)S(1)}, f32[128,128]{1,0:T(8,128)S(1)}, s32[]{:T(128)}) %tuple.79), condition=%wide.region_9.9_spmd.clone, body=%wide.region_6.8_spmd.clone.sunk | while | flops 198145 | bytes 336977 | solution.py:64
  1142.8 1.2 fusion.40
  1144.0 1.9 convolution_subtract_fusion.2
  1145.9 1.7 fusion.41
  1147.6 1.0 broadcast_in_dim.74
  1148.6 44.9 %all_to_all.10 = f32[8,128,256]{2,1,0:T(8,128)S(1)} all-to-all(f32[8,128,256]{2,1,0:T(8,128)S(1)} %broadcast_in_dim.74), channel_id=1, replica_groups=mesh['layer'=8,'row'=4,'col'=16] {'layer'}, dimensions={0} | all-to-all | bytes 2097152 | tf_op jit(solution)/shard_map/all_to_all | solution.py:34
  1193.4 1.0 copy.22
  (1823 shorter events, 519.2 us)
Async XLA Ops:
  6.5 47.0 %all-to-all-start = ((f32[8,128,256]{2,1,0:T(8,128)}), f32[8,128,256]{2,1,0:T(8,128)S(1)}, u32[]{:S(2)}, u32[]{:S(2)}) async-start(f32[8,128,256]{2,1,0:T(8,128)} %bitcast.51), calls=%async_computation | async-start | bytes 2097152 | tf_op jit(solution)/shard_map/all_to_all | solution.py:18
  54.3 183.4 %all-gather.10.cloned.1.call-start = ((), (), s32[]{:S(2)}) async-start(), calls=%async_computation.2 | async-start | bytes 4325376 | tf_op jit(solution)/shard_map/while/body/eval_jaxpr/all_gather | solution.py:23
  55.0 287.3 %all-gather.12.cloned.1.call-start = ((), (), s32[]{:S(2)}) async-start(), calls=%async_computation.3 | async-start | bytes 1114112 | tf_op jit(solution)/shard_map/while/body/eval_jaxpr/all_gather | solution.py:23
  239.4 368.2 %all-gather.14.cloned.1.call-start = ((), (), s32[]{:S(2)}) async-start(), calls=%async_computation.4 | async-start | bytes 1114112 | tf_op jit(solution)/shard_map/while/body/eval_jaxpr/all_gather | solution.py:23
  611.2 163.0 %all-gather.10.cloned.1.call-start = ((), (), s32[]{:S(2)}) async-start(), calls=%async_computation.2 | async-start | bytes 4325376 | tf_op jit(solution)/shard_map/while/body/eval_jaxpr/all_gather | solution.py:23
  611.8 266.9 %all-gather.12.cloned.1.call-start = ((), (), s32[]{:S(2)}) async-start(), calls=%async_computation.3 | async-start | bytes 1114112 | tf_op jit(solution)/shard_map/while/body/eval_jaxpr/all_gather | solution.py:23
  775.9 368.1 %all-gather.14.cloned.1.call-start = ((), (), s32[]{:S(2)}) async-start(), calls=%async_computation.4 | async-start | bytes 1114112 | tf_op jit(solution)/shard_map/while/body/eval_jaxpr/all_gather | solution.py:23
Sparse Core Ops, SparseCore 0:
  59.4 178.3 all-gather.9
  239.8 102.4 all-gather.11
  344.4 99.4 all-gather.13
  616.0 158.1 all-gather.9
  776.2 102.4 all-gather.11
  880.6 99.5 all-gather.13
where the time goes:
time: 1210 us; the launch traced here: 1200 us
  waiting for transfers between devices  567 us (47%)
  other arithmetic  516 us (43%)
  blocking collectives  44.9 us (4%)
  loops' own time  19.6 us (2%)
  starting transfers between devices  18.4 us (2%)
  between operations  13.4 us (1%)
  local copies, waits for them, and re-layouts  12.3 us (1%)
    all_gather x6, waiting for transfers between devices, from_root(): lax.all_gather(array, axis)  540 us
    reduce_sum x256, other arithmetic, sweep(): pivot = jnp.sum(mat_row * unit)  153 us
    mul x256, other arithmetic, sweep(): inv = inv - column[:, None] * inv_row[None, :]  147 us
    mul x256, other arithmetic, sweep(): mat = mat - column[:, None] * mat_row[None, :]  147 us
    all_to_all x1, blocking collectives, copy_for_each(): lax.all_to_all(jnp.broadcast_to(array[None], (count, *array.shape)), axis...  44.9 us
    add x256, other arithmetic, sweep(): inv = inv * keep + unit[:, None] * inv_row[None, :]  35.7 us
    reduce_sum x256, other arithmetic, sweep(): column = jnp.sum(mat * unit[None, :], axis=1) * (1.0 - unit)  26.5 us
    all_to_all x1, waiting for transfers between devices, sum_at_owner(): parts = lax.all_to_all(split_up(array, dim, count), axis, 0, 0, tiled=True)  25.8 us
  transfers between devices with their start and end apart: 7, of which 5 were waited for; matrix products, arithmetic and copies ran while one was open for 44% of the time, Pallas kernels for 0%

commit v1 on v0

v1 whole, which is shorter than its diff:
```python
import functools

import jax
import jax.numpy as jnp
from jax import lax
from jax.experimental import pallas as pl
from jax.experimental.pallas import tpu as pltpu
from jax.sharding import PartitionSpec as P

MESH = pl.DeviceIdType.MESH
NB = 128
F32 = jnp.float32
PART = 224
SPLIT_B = (112, 112)
SPLIT_C = (112, 112)


def dev(y, z, x, k):
    y, z, x = lax.rem(y + 8, 4), lax.rem(z + 32, 16), lax.rem(x + 8, 4)
    return (y * 2 + z // 8, x, lax.rem(z, 8) * 2 + k)


def dot(a, b):
    return jnp.dot(a, b, precision=lax.Precision.HIGHEST, preferred_element_type=F32)


def inverse_steps(v, lo, hi):
    n = NB
    lane8 = lax.broadcasted_iota(jnp.int32, (8, n), 1)
    sub8 = lax.broadcasted_iota(jnp.int32, (8, n), 0)
    subc = lax.broadcasted_iota(jnp.int32, (8, 8, n), 1)
    colc = lax.broadcasted_iota(jnp.int32, (8, 8, n), 0)
    lane = lax.broadcasted_iota(jnp.int32, (n, n), 1)
    for b in range(lo, hi):
        o = b * 8
        v0 = v[o : o + 8, :]
        c = jnp.stack([jnp.broadcast_to(v0[:, o + s : o + s + 1], (8, n)) for s in range(8)])
        for s in range(8):
            row = c[:, s : s + 1, :]
            pinv = 1.0 / row[s : s + 1]
            row = jnp.where(colc[:, :1] == s, pinv, row * pinv)
            base = jnp.where(colc == s, 0.0, c)
            c = jnp.where(subc == s, jnp.broadcast_to(row, (8, 8, n)), base - c[s : s + 1] * row)
        eye = (lane8 - o == sub8).astype(F32)
        v0 = jnp.where((lane8 >= o) & (lane8 < o + 8), eye, v0)
        r = c[0] * v0[0:1]
        for s in range(1, 8):
            r = r + c[s] * v0[s : s + 1]
        acc = jnp.where((lane >= o) & (lane < o + 8), 0.0, v)
        for s in range(8):
            acc = acc - v[:, o + s : o + s + 1] * r[s : s + 1]
        parts = [acc[:o]] if o else []
        parts += [r, acc[o + 8 :]] if o + 8 < n else [r]
        v = jnp.concatenate(parts, 0)
    return v


class Chunk:
    def __init__(self, base, stride, off, rows, lo, hi, recv, part, far):
        self.base, self.stride, self.off, self.rows = base, stride, off, rows
        self.cols = slice(lo, hi)
        self.recv, self.part, self.far = recv, part, far

    def at(self, ref, y):
        start = pl.multiple_of(self.base + y * self.stride + self.off, 8)
        return ref.at[pl.ds(start, self.rows), self.cols]

    def xrows(self, ref, k, y):
        start = pl.multiple_of(self.base + y * self.stride + self.off, 8)
        return ref.at[k, pl.ds(start, self.rows)]

    def mine(self, ref, *lead):
        return ref.at[(*lead, slice(self.off, self.off + self.rows))]


def kernel(
    order_ref, t_hbm, o_hbm,
    t, f, u, ra, rb, rc, pa, pb, pc, za, zb, zc, xa, dx, yb, xf, mat,
    in_sem, out_sem, ssem, rsem,
):
    layer, x, col = lax.axis_index("layer"), lax.axis_index("row"), lax.axis_index("col")
    y, zl, k = layer // 2, col // 2, lax.rem(col, 2)
    z = lax.rem(layer, 2) * 8 + zl
    count = [0]
    sends = []

    def new():
        count[0] += 1
        return count[0] - 1

    def copy(i, src, dst, target, j=None):
        return pltpu.make_async_remote_copy(
            src_ref=src, dst_ref=dst, send_sem=ssem.at[i],
            recv_sem=rsem.at[i if j is None else j], device_id=target, device_id_type=MESH,
        )

    def start(c, cond=None):
        if cond is None:
            c.start()
        else:
            pl.when(cond)(c.start)
        sends.append((c, cond))

    a = Chunk(0, 32, 0, 32, 0, 256, ra, pa, za)
    bs, cs, off = [], [], 0
    for n in SPLIT_B:
        bs.append(Chunk(NB, PART, off, n, 0, 128, rb, pb, zb))
        off += n
    off = 0
    for n in SPLIT_C:
        cs.append(Chunk(NB, PART, off, n, 128, 256, rc, pc, zc))
        off += n
    chunks = [a, *bs, *cs]

    loads = [
        pltpu.make_async_copy(t_hbm.at[r, c], t.at[r, c], in_sem.at[i])
        for i, (r, c) in enumerate(
            [
                (slice(0, 128), slice(0, 256)),
                (slice(128, 1024), slice(0, 128)),
                (slice(128, 1024), slice(128, 256)),
            ]
        )
    ]
    for c in loads:
        c.start()

    barrier = pltpu.get_barrier_semaphore()
    peers = [dev(y + i, z, x + j, k) for i in range(4) for j in range(4) if i or j]
    peers += [dev(y, z + d, x, k) for d in (8, 1, 2, 3, 4, -1, -2, -3, -4)]
    peers += [dev(y, z, x, 1 - k)]
    for p in peers:
        pl.semaphore_signal(barrier, inc=1, device_id=p, device_id_type=MESH)
    pl.semaphore_wait(barrier, len(peers))

    rs = {}
    for n, c in enumerate(chunks):
        if n in (0, 1, 1 + len(bs)):
            loads[0 if n == 0 else 1 if n == 1 else 2].wait()
        for d in (1, 3, 2):
            y2 = lax.rem(y + d, 4)
            rs[c, d] = copy(new(), c.at(t, y2), c.mine(c.recv, d - 1), dev(y2, z, x, k))
            start(rs[c, d])
    zx = {}
    for c in chunks:
        for d in (1, 2, 3):
            rs[c, d].wait_recv()
        own, got = c.at(t, y), [c.mine(c.recv, d)[...] for d in range(3)]
        c.mine(c.part)[...] = (own[...] + got[0]) + (got[1] + got[2])
        zx[c] = copy(new(), c.mine(c.part), c.mine(c.far), dev(y, z + 8, x, k))
        start(zx[c])

    ag = {}

    def gather_rows(c):
        zx[c].wait_recv()
        s = c.mine(c.part)[...] + c.mine(c.far)[...]
        c.at(f, y)[...] = s
        return s

    def send_rows(c):
        for d in (1, 3, 2):
            ag[c, d] = copy(new(), c.at(f, y), c.at(f, y), dev(y + d, z, x, k))
            start(ag[c, d])

    s = gather_rows(a)

    @pl.when(zl == 0)
    def _():
        xa[...] = s[:, :128]

    j = new()
    for i, d in enumerate((1, -1, 2, -2, 3, -3, 4)):
        c4 = copy(j if i == 0 else new(), xa, xa, dev(y, z + d, x, k), j)
        start(c4, zl == 0)

    slot = jnp.minimum(x, 2)
    rows_y = pl.ds(pl.multiple_of(y * 32, 8), 32)
    panel = x < 2
    rows_of = {}

    def plane_rows():
        for dxx in (1, 3, 2):
            for dy in range(4):
                rows_of[dxx, dy] = copy(
                    new(), f.at[rows_y], yb.at[jnp.minimum(x, 1), rows_y],
                    dev(y + dy, z, x + dxx, k),
                )
                start(rows_of[dxx, dy], panel)

    send_rows(a)
    plane_rows()

    @pl.when(zl != 0)
    def _():
        copy(j, xa, xa, dev(y, z, x, 1 - k)).wait_recv()

    plane = {}
    for dxx in (0, 1, 3, 2):
        for dy in (0, 1, 3, 2):
            if dxx or dy:
                plane[dxx, dy] = copy(
                    new(), xa, dx.at[slot, k, rows_y], dev(y + dy, z, x + dxx, k)
                )
                start(plane[dxx, dy], panel if dxx else None)
    dx[slot, k, rows_y] = xa[...]

    tree = {}
    xg = {}

    def tree_send(c):
        jt = new()
        here = c.xrows(xf, k, y)
        tree[c] = copy(jt, here, here, dev(y, z, x, 1 - k))
        idx = [jt, new(), new(), new()]
        for i, d in zip(idx, (2, -2, 1, -1)):
            start(copy(i, here, here, dev(y, z + d, x, k), jt), zl == 0)
        return idx

    def tree_pass(c, idx):
        here = c.xrows(xf, k, y)
        jt = idx[0]

        @pl.when(zl != 0)
        def _():
            tree[c].wait_recv()

        start(copy(idx[0], here, here, dev(y, z + 2, x, k), jt), zl == 2)
        start(copy(idx[1], here, here, dev(y, z + 1, x, k), jt), zl == 2)
        start(copy(idx[0], here, here, dev(y, z - 1, x, k), jt), zl == 6)
        for d in (1, 3, 2):
            xg[c, d] = copy(new(), here, here, dev(y + d, z, x, k))
            start(xg[c, d])

    tree_idx = {}

    def columns(c):
        s = gather_rows(c)

        @pl.when(zl == 0)
        def _():
            c.xrows(xf, k, y)[...] = s

        tree_idx[c] = tree_send(c)
        send_rows(c)

    columns(bs[0])

    for dxx in range(4):
        for dy in range(4):
            if dxx or dy:
                if dxx:
                    cond = lax.rem(x - dxx + 4, 4) < 2
                    pl.when(cond)(plane[dxx, dy].wait_recv)
                else:
                    plane[dxx, dy].wait_recv()
    sib = copy(new(), dx.at[0:2, k], dx.at[0:2, k], dev(y, z, x, 1 - k))
    start(sib)
    sib2 = copy(new(), dx.at[2, k], dx.at[2, k], dev(y, z, x, 1 - k))
    start(sib2, x >= 2)
    sib.wait_recv()

    first = order_ref[0]
    swapped = jnp.full((NB, NB), first, jnp.int32) == 1
    d00, d01, d10, d11 = dx[0, 0], dx[0, 1], dx[1, 0], dx[1, 1]
    dpp, dqq = jnp.where(swapped, d11, d00), jnp.where(swapped, d00, d11)
    dpq, dqp = jnp.where(swapped, d10, d01), jnp.where(swapped, d01, d10)

    mat[0] = inverse_steps(dpp, 0, 8)
    tree_pass(bs[0], tree_idx[bs[0]])
    for c in bs[1:]:
        columns(c)
    mat[0] = inverse_steps(mat[0], 8, 16)
    pinv = mat[0]
    w = dot(pinv, dpq)
    v = dot(dqp, pinv)
    mat[1] = dqq - dot(dqp, w)
    for c in bs[1:]:
        tree_pass(c, tree_idx[c])
    mat[1] = inverse_steps(mat[1], 0, 8)
    for c in cs[:-1]:
        gather_rows(c)
        send_rows(c)
    mat[1] = inverse_steps(mat[1], 8, 16)
    for c in cs[-1:]:
        gather_rows(c)
        send_rows(c)
    qinv = mat[1]

    for d in (1, 2, 3):
        ag[a, d].wait_recv()
    for (dxx, dy), c in rows_of.items():
        pl.when(lax.rem(x - dxx + 4, 4) < 2)(c.wait_recv)
    for i in range(2):

        @pl.when(x == i)
        def _(i=i):
            yb[i] = f[0:NB, :]

    def full(value):
        return jnp.full((NB, 256), value, jnp.int32)

    wide = full(first) == 1
    y0, y1 = yb[0], yb[1]
    yp, yq = jnp.where(wide, y1, y0), jnp.where(wide, y0, y1)
    tp = dot(pinv, yp)
    gq = dot(qinv, yq - dot(v, yp))
    gp = tp - dot(w, gq)
    left = lax.broadcasted_iota(jnp.int32, (NB, 256), 1) < NB
    here = left & (full(zl) == 0)
    is_p = here & (full(first) == full(k))
    is_q = here & (full(first) != full(k))
    zero = jnp.zeros((NB, NB), F32)
    pad_p = jnp.concatenate([pinv, zero], 1)
    pad_q = jnp.concatenate([qinv, zero], 1)
    pad_wq = jnp.concatenate([dot(w, qinv), zero], 1)
    gp = jnp.where(is_p, -pad_p, jnp.where(is_q, pad_wq, gp))
    gq = jnp.where(is_p, 0.0, jnp.where(is_q, -pad_q, gq))
    row_p = full(first) == full(x)
    row_q = (full(x) < 2) & (full(first) != full(x))
    gp0 = jnp.where(row_p, 0.0, jnp.where(row_q, jnp.where(is_p, -pad_p, tp), gp))
    gq0 = jnp.where(row_p | row_q, 0.0, gq)
    drop0 = (is_p & ~row_p) | (is_q & ~row_p & ~row_q)
    drop = is_p | is_q

    def stacked(p, q):
        return jnp.concatenate([jnp.where(wide, q, p), jnp.where(wide, p, q)], 0)

    g0, g = stacked(gp0, gq0), stacked(gp, gq)

    pl.when(x >= 2)(sib2.wait_recv)
    x0 = jnp.concatenate([dx[slot, 0], dx[slot, 1]], 1)
    u[0:NB, :] = jnp.where(drop0, 0.0, f[0:NB, :]) - dot(x0, g0)

    for c in xg.values():
        c.wait_recv()
    xs = copy(new(), xf.at[k, NB:], xf.at[k, NB:], dev(y, z, x, 1 - k))
    start(xs)
    xs.wait_recv()
    for n in range(7):
        r = slice(NB + n * NB, 2 * NB + n * NB)
        u[r, :] = dot(jnp.concatenate([xf[0, r], xf[1, r]], 1), g)
    for c in chunks[1:]:
        for d in (1, 2, 3):
            ag[c, d].wait_recv()
    for n in range(7):
        r = slice(NB + n * NB, 2 * NB + n * NB)
        u[r, :] = jnp.where(drop, 0.0, f[r, :]) - u[r, :]
    out = pltpu.make_async_copy(u, o_hbm, out_sem.at[0])
    out.start()
    for c, cond in sends:
        if cond is None:
            c.wait_send()
        else:
            pl.when(cond)(c.wait_send)
    out.wait()


def solution(mesh):
    rows, cols = 1024, 256

    def body(terms, order):
        vm = lambda *s: pltpu.VMEM(s, F32)
        return pl.pallas_call(
            kernel,
            out_shape=jax.ShapeDtypeStruct((rows, cols), F32),
            in_specs=[
                pl.BlockSpec(memory_space=pltpu.SMEM),
                pl.BlockSpec(memory_space=pl.ANY),
            ],
            out_specs=pl.BlockSpec(memory_space=pl.ANY),
            scratch_shapes=[
                vm(rows, cols), vm(rows, cols), vm(rows, cols),
                vm(3, 32, 256), vm(3, PART, 128), vm(3, PART, 128),
                vm(32, 256), vm(PART, 128), vm(PART, 128),
                vm(32, 256), vm(PART, 128), vm(PART, 128),
                vm(32, 128), vm(3, 2, 128, 128), vm(2, 128, 256), vm(2, rows, 128), vm(2, 128, 128),
                pltpu.SemaphoreType.DMA((3,)),
                pltpu.SemaphoreType.DMA((1,)),
                pltpu.SemaphoreType.DMA((128,)),
                pltpu.SemaphoreType.DMA((128,)),
            ],
            compiler_params=pltpu.CompilerParams(collective_id=0, has_side_effects=True),
            name="front",
        )(order, terms.reshape(rows, cols))

    return jax.shard_map(
        body,
        mesh=mesh,
        in_specs=(P("layer", "row", "col"), P()),
        out_specs=P("row", "col"),
        check_vma=False,
    )
```

time: 1210 us -> 76.4 us (0.06)
  the two profiles are of different devices: /device:TPU:1 before, /device:TPU:103 now
where the time goes in v1:
time: 76.4 us; the launch traced here: 76.3 us
  Pallas kernels  74 us (97%)
  local copies, waits for them, and re-layouts  2.26 us (3%)
    pallas_call x1, Pallas kernels, body(): pl.pallas_call(kernel, out_shape=jax.ShapeDtypeStruct((rows, cols), F32),...  74 us
    unnamed x1, local copies, waits for them, and re-layouts  2.26 us

profile of v1, /device:TPU:103, one launch (start us, length us, event | category | flops | bytes accessed | tf_op | source)
XLA Modules:
  0.0 76.3 jit_solution(11069290160358870993)
XLA Ops:
  0.0 74.0 %front.1 = f32[1024,256]{1,0:T(8,128)} custom-call(s32[2]{0:T(128)} %order_ref.1, f32[1024,256]{1,0:T(8,128)} %bitcast.1), custom_call_target="tpu_custom_call" | custom-call | tf_op jit(solution)/shard_map/front/pallas_call | solution.py:364
  74.0 2.3 %copy.4 = f32[1024,256]{1,0:T(8,128)} copy(f32[1024,256]{1,0:T(8,128)} %front.1) | data formatting | bytes 2097152

commit v2 on v1

v2 whole, which is shorter than its diff:
```python
import functools

import jax
import jax.numpy as jnp
from jax import lax
from jax.experimental import pallas as pl
from jax.experimental.pallas import tpu as pltpu
from jax.sharding import PartitionSpec as P

MESH = pl.DeviceIdType.MESH
NB = 128
F32 = jnp.float32
PART = 224
SPLIT = (112, 112)


def dev(y, z, x, k):
    y, z, x = lax.rem(y + 8, 4), lax.rem(z + 32, 16), lax.rem(x + 8, 4)
    return (y * 2 + z // 8, x, lax.rem(z, 8) * 2 + k)


def dot(a, b):
    return jnp.dot(a, b, precision=lax.Precision.HIGHEST, preferred_element_type=F32)


def inverse_steps(v, lo, hi):
    n = NB
    lane8 = lax.broadcasted_iota(jnp.int32, (8, n), 1)
    sub8 = lax.broadcasted_iota(jnp.int32, (8, n), 0)
    subc = lax.broadcasted_iota(jnp.int32, (8, 8, n), 1)
    colc = lax.broadcasted_iota(jnp.int32, (8, 8, n), 0)
    lane = lax.broadcasted_iota(jnp.int32, (n, n), 1)
    for b in range(lo, hi):
        o = b * 8
        v0 = v[o : o + 8, :]
        c = jnp.stack([jnp.broadcast_to(v0[:, o + s : o + s + 1], (8, n)) for s in range(8)])
        for s in range(8):
            row = c[:, s : s + 1, :]
            pinv = 1.0 / row[s : s + 1]
            row = jnp.where(colc[:, :1] == s, pinv, row * pinv)
            base = jnp.where(colc == s, 0.0, c)
            c = jnp.where(subc == s, jnp.broadcast_to(row, (8, 8, n)), base - c[s : s + 1] * row)
        eye = (lane8 - o == sub8).astype(F32)
        v0 = jnp.where((lane8 >= o) & (lane8 < o + 8), eye, v0)
        r = c[0] * v0[0:1]
        for s in range(1, 8):
            r = r + c[s] * v0[s : s + 1]
        acc = jnp.where((lane >= o) & (lane < o + 8), 0.0, v)
        for s in range(8):
            acc = acc - v[:, o + s : o + s + 1] * r[s : s + 1]
        parts = [acc[:o]] if o else []
        parts += [r, acc[o + 8 :]] if o + 8 < n else [r]
        v = jnp.concatenate(parts, 0)
    return v


class Chunk:
    def __init__(self, base, stride, off, rows, lo, hi, recv, part, far):
        self.base, self.stride, self.off, self.rows = base, stride, off, rows
        self.cols = slice(lo, hi)
        self.sub = slice(off, off + rows)
        self.recv, self.part, self.far = recv, part, far

    def at(self, ref, y):
        start = pl.multiple_of(self.base + y * self.stride + self.off, 8)
        return ref.at[pl.ds(start, self.rows), self.cols]

    def mine(self, ref, *lead):
        return ref.at[(*lead, self.sub)]


def kernel(
    order_ref, t_hbm, o_hbm,
    t, f, u, ra, rb, rc, pa, pb, pc, za, zb, zc, xh, xa, dx, yb, xf, mat,
    in_sem, out_sem, ssem, rsem,
):
    layer, x, col = lax.axis_index("layer"), lax.axis_index("row"), lax.axis_index("col")
    y, zl, k = layer // 2, col // 2, lax.rem(col, 2)
    zh = lax.rem(layer, 2)
    z = zh * 8 + zl
    source, relay = zl == 0, (zl == 2) | (zl == 6)
    other = dev(y, z, x, 1 - k)
    count = [0]
    sends = []

    def new():
        count[0] += 1
        return count[0] - 1

    def copy(i, src, dst, target, j=None):
        return pltpu.make_async_remote_copy(
            src_ref=src, dst_ref=dst, send_sem=ssem.at[i],
            recv_sem=rsem.at[i if j is None else j], device_id=target, device_id_type=MESH,
        )

    def start(c, cond=None):
        if cond is None:
            c.start()
        else:
            pl.when(cond)(c.start)
        sends.append((c, cond))

    a = Chunk(0, 32, 0, 32, 0, 256, ra, pa, za)
    bs, cs, off = [], [], 0
    for n in SPLIT:
        bs.append(Chunk(NB, PART, off, n, 0, 128, rb, pb, zb))
        cs.append(Chunk(NB, PART, off, n, 128, 256, rc, pc, zc))
        off += n
    chunks = [a, *bs, *cs]

    loads = [
        pltpu.make_async_copy(t_hbm.at[r, c], t.at[r, c], in_sem.at[i])
        for i, (r, c) in enumerate(
            [
                (slice(0, 128), slice(0, 256)),
                (slice(128, 1024), slice(0, 128)),
                (slice(128, 1024), slice(128, 256)),
            ]
        )
    ]
    for c in loads:
        c.start()

    barrier = pltpu.get_barrier_semaphore()
    peers = [dev(y + i, z, x + j, k) for i in range(4) for j in range(4) if i or j]
    peers += [dev(y, z + d, x, k) for d in range(1, 16)]
    peers += [other]
    for p in peers:
        pl.semaphore_signal(barrier, inc=1, device_id=p, device_id_type=MESH)
    pl.semaphore_wait(barrier, len(peers))

    rs, zx = {}, {}
    for n, c in enumerate(chunks):
        if n in (0, 1, 1 + len(bs)):
            loads[0 if n == 0 else 1 if n == 1 else 2].wait()
        for d in (1, 3, 2):
            y2 = lax.rem(y + d, 4)
            rs[c, d] = copy(new(), c.at(t, y2), c.mine(c.recv, d - 1), dev(y2, z, x, k))
            start(rs[c, d])

    def half_sum(c):
        for d in (1, 2, 3):
            rs[c, d].wait_recv()
        own, got = c.at(t, y), [c.mine(c.recv, d)[...] for d in range(3)]
        c.mine(c.part)[...] = (own[...] + got[0]) + (got[1] + got[2])
        zx[c] = copy(new(), c.mine(c.part), c.mine(c.far), dev(y, z + 8, x, k))
        sends.append((zx[c], None))

    def full_sum(c):
        zx[c].wait_recv()
        return c.mine(c.part)[...] + c.mine(c.far)[...]

    half_sum(a)
    xhalf = {}
    for d in (1, 15, 2, 14, 3, 13, 4, 12, 5, 11, 6, 10, 7, 9, 8):
        i = new()
        if not xhalf:
            xhalf[0], xhalf[1] = i, new()
        for h in range(2):
            c = copy(i, pa.at[:, :128], xh.at[h], dev(y, z + d, x, k), xhalf[h])
            start(c, source & (zh == h))
    panel = x < 2
    plain, inner = jnp.logical_not(panel), jnp.logical_not(source)
    leaf = jnp.logical_not(source | relay)
    pl.when(plain & inner)(zx[a].start)
    half_sum(bs[0])
    pl.when(panel & inner)(zx[a].start)
    pl.when(plain)(zx[bs[0]].start)
    for c in bs[1:]:
        half_sum(c)
    pl.when(panel)(zx[bs[0]].start)
    for c in bs[1:]:
        zx[c].start()
    pl.when(source)(zx[a].start)
    half_sum(cs[0])
    pl.when(leaf)(zx[cs[0]].start)

    slot = jnp.minimum(x, 2)
    rows_y = pl.ds(pl.multiple_of(y * 32, 8), 32)
    plane = {(i, j): new() for i in (0, 1, 3, 2) for j in (0, 1, 3, 2) if i or j}

    def across(i, j):
        return copy(plane[i, j], xa, dx.at[slot, k, rows_y], dev(y + j, z, x + i, k))

    def columns(cond):
        for h in range(2):

            @pl.when(cond & source & (zh == h))
            def _(h=h):
                xh[h] = pa[:, :128]

            @pl.when(cond & jnp.logical_not(source & (zh == h)))
            def _(h=h):
                copy(xhalf[h], xh.at[h], xh.at[h], other).wait_recv()

        @pl.when(cond)
        def _():
            xa[...] = xh[0] + xh[1]
            dx[slot, k, rows_y] = xa[...]

        for i, j in plane:
            if cond is panel or not i:
                start(across(i, j), cond)

    columns(panel)
    for c in cs[1:]:
        half_sum(c)
        pl.when(leaf)(zx[c].start)

    f[rows_y, :] = full_sum(a)
    ag = {}
    for d in (1, 3, 2):
        ag[a, d] = copy(new(), f.at[rows_y], f.at[rows_y], dev(y + d, z, x, k))
        start(ag[a, d])
    rows_of = {}
    for dxx in (1, 3, 2):
        for dy in range(4):
            rows_of[dxx, dy] = copy(
                new(), f.at[rows_y], yb.at[jnp.minimum(x, 1), rows_y],
                dev(y + dy, z, x + dxx, k),
            )
            start(rows_of[dxx, dy], panel)

    branch, xg = {}, {}

    def spread(c, cond):
        for d in (1, 3, 2):
            pl.when(cond)(xg[c, d].start)

    def gather(c):
        zx[c].wait_recv()
        total = c.mine(c.part)[...] + c.mine(c.far)[...]
        if c in bs:
            here = c.mine(xf, k, y)
            branch[c] = [new() for _ in range(4)]
            for d in (1, 3, 2):
                xg[c, d] = copy(new(), here, here, dev(y + d, z, x, k))
                sends.append((xg[c, d], None))

            @pl.when(source)
            def _():
                here[...] = total

            for i, d in zip(branch[c], (2, -2, 1, -1)):
                start(copy(i, here, here, dev(y, z + d, x, k), branch[c][0]), source)
            spread(c, source)
            total = jnp.where(jnp.full((c.rows, 128), zl, jnp.int32) == 0, 0.0, total)
        c.at(f, y)[...] = total
        for d in (1, 3, 2):
            ag[c, d] = copy(new(), c.at(f, y), c.at(f, y), dev(y + d, z, x, k))
            start(ag[c, d])

    def pass_on(c, cond):
        here = c.mine(xf, k, y)
        i, i2 = branch[c][:2]

        @pl.when(cond)
        def _():
            copy(i, here, here, other).wait_recv()

        if cond is relay:
            start(copy(i, here, here, dev(y, z + 2, x, k), i), zl == 2)
            start(copy(i2, here, here, dev(y, z + 1, x, k), i), zl == 2)
            start(copy(i, here, here, dev(y, z - 1, x, k), i), zl == 6)
        spread(c, cond)

    for i, j in plane:
        pl.when(lax.rem(x - i + 4, 4) < 2)(across(i, j).wait_recv)
    gather(bs[0])
    pl.when(source)(zx[cs[0]].start)
    sib = copy(new(), dx.at[0:2, k], dx.at[0:2, k], other)
    start(sib)
    sib2 = copy(new(), dx.at[2, k], dx.at[2, k], other)
    sib.wait_recv()

    first = order_ref[0]
    swapped = jnp.full((NB, NB), first, jnp.int32) == 1
    d00, d01, d10, d11 = dx[0, 0], dx[0, 1], dx[1, 0], dx[1, 1]
    dpp, dqq = jnp.where(swapped, d11, d00), jnp.where(swapped, d00, d11)
    dpq, dqp = jnp.where(swapped, d10, d01), jnp.where(swapped, d01, d10)

    mat[0] = inverse_steps(dpp, 0, 8)
    pass_on(bs[0], relay)
    pl.when(relay)(zx[cs[0]].start)
    for c in bs[1:]:
        gather(c)
    for c in cs[1:]:
        pl.when(source)(zx[c].start)
    mat[0] = inverse_steps(mat[0], 8, 16)
    pinv = mat[0]
    w = dot(pinv, dpq)
    v = dot(dqp, pinv)
    mat[1] = dqq - dot(dqp, w)
    mat[1] = inverse_steps(mat[1], 0, 8)
    for c in bs[1:]:
        pass_on(c, relay)
    for c in cs[1:]:
        pl.when(relay)(zx[c].start)
    mat[1] = inverse_steps(mat[1], 8, 16)
    qinv = mat[1]
    columns(plain)

    for d in (1, 2, 3):
        ag[a, d].wait_recv()
    for (dxx, dy), c in rows_of.items():
        pl.when(lax.rem(x - dxx + 4, 4) < 2)(c.wait_recv)
    for i in range(2):

        @pl.when(x == i)
        def _(i=i):
            yb[i] = f[0:NB, :]

    def full(value):
        return jnp.full((NB, 256), value, jnp.int32)

    wide = full(first) == 1
    y0, y1 = yb[0], yb[1]
    yp, yq = jnp.where(wide, y1, y0), jnp.where(wide, y0, y1)
    tp = dot(pinv, yp)
    gq = dot(qinv, yq - dot(v, yp))
    gp = tp - dot(w, gq)
    left = lax.broadcasted_iota(jnp.int32, (NB, 256), 1) < NB
    here = left & (full(zl) == 0)
    is_p = here & (full(first) == full(k))
    is_q = here & (full(first) != full(k))
    zero = jnp.zeros((NB, NB), F32)
    pad_p = jnp.concatenate([pinv, zero], 1)
    pad_q = jnp.concatenate([qinv, zero], 1)
    pad_wq = jnp.concatenate([dot(w, qinv), zero], 1)
    gp = jnp.where(is_p, -pad_p, jnp.where(is_q, pad_wq, gp))
    gq = jnp.where(is_p, 0.0, jnp.where(is_q, -pad_q, gq))
    row_p = full(first) == full(x)
    row_q = (full(x) < 2) & (full(first) != full(x))
    gp0 = jnp.where(row_p, 0.0, jnp.where(row_q, jnp.where(is_p, -pad_p, tp), gp))
    gq0 = jnp.where(row_p | row_q, 0.0, gq)
    drop0 = (is_p & ~row_p) | (is_q & ~row_p & ~row_q)

    def stacked(p, q):
        return jnp.concatenate([jnp.where(wide, q, p), jnp.where(wide, p, q)], 0)

    g0, g = stacked(gp0, gq0), stacked(gp, gq)

    for j in range(1, 4):
        pl.when(plain)(across(0, j).wait_recv)
    start(sib2, plain)
    for c in cs[:-1]:
        gather(c)
    pl.when(plain)(sib2.wait_recv)
    x0 = jnp.concatenate([dx[slot, 0], dx[slot, 1]], 1)
    u[0:NB, :] = jnp.where(drop0, 0.0, f[0:NB, :]) - dot(x0, g0)
    outs = []

    def put(r, cols):
        outs.append(pltpu.make_async_copy(u.at[r, cols], o_hbm.at[r, cols], out_sem.at[len(outs)]))
        outs[-1].start()

    put(slice(0, NB), slice(0, 256))
    side = {}
    pass_on(bs[0], leaf)
    gather(cs[-1])
    for c in bs[1:]:
        pass_on(c, leaf)
    for c in bs:
        for d in (1, 2, 3):
            xg[c, d].wait_recv()
        here = xf.at[k, :, c.sub]
        side[c] = copy(new(), here, here, other)
        start(side[c])
    for c in bs:
        side[c].wait_recv()
    for i in range(4):
        u[NB + i * PART : NB + (i + 1) * PART, :] = dot(
            jnp.concatenate([xf[0, i], xf[1, i]], 1), g
        )
    for c in chunks[1:]:
        for d in (1, 2, 3):
            ag[c, d].wait_recv()
        for i in range(4):
            r = slice(NB + i * PART + c.off, NB + i * PART + c.off + c.rows)
            u[r, c.cols] = f[r, c.cols] - u[r, c.cols]
            put(r, c.cols)
    for c, cond in sends:
        if cond is None:
            c.wait_send()
        else:
            pl.when(cond)(c.wait_send)
    for c in outs:
        c.wait()


def solution(mesh):
    rows, cols = 1024, 256

    def body(terms, order):
        vm = lambda *s: pltpu.VMEM(s, F32)
        return pl.pallas_call(
            kernel,
            out_shape=jax.ShapeDtypeStruct((rows, cols), F32),
            in_specs=[
                pl.BlockSpec(memory_space=pltpu.SMEM),
                pl.BlockSpec(memory_space=pl.ANY),
            ],
            out_specs=pl.BlockSpec(memory_space=pl.ANY),
            scratch_shapes=[
                vm(rows, cols), vm(rows, cols), vm(rows, cols),
                vm(3, 32, 256), vm(3, PART, 128), vm(3, PART, 128),
                vm(32, 256), vm(PART, 128), vm(PART, 128),
                vm(32, 256), vm(PART, 128), vm(PART, 128),
                vm(2, 32, 128), vm(32, 128), vm(3, 2, 128, 128), vm(2, 128, 256),
                vm(2, 4, PART, 128), vm(2, 128, 128),
                pltpu.SemaphoreType.DMA((3,)),
                pltpu.SemaphoreType.DMA((1 + 8 * len(SPLIT),)),
                pltpu.SemaphoreType.DMA((128,)),
                pltpu.SemaphoreType.DMA((128,)),
            ],
            compiler_params=pltpu.CompilerParams(collective_id=0, has_side_effects=True),
            name="front",
        )(order, terms.reshape(rows, cols))

    return jax.shard_map(
        body,
        mesh=mesh,
        in_specs=(P("layer", "row", "col"), P()),
        out_specs=P("row", "col"),
        check_vma=False,
    )
```

time: 76.4 us -> 72.5 us (0.949)
  the two profiles are of different devices: /device:TPU:103 before, /device:TPU:72 now
where the time goes in v2:
time: 72.5 us; the launch traced here: 72.4 us
  Pallas kernels  70.1 us (97%)
  local copies, waits for them, and re-layouts  2.26 us (3%)
    pallas_call x1, Pallas kernels, body(): pl.pallas_call(kernel, out_shape=jax.ShapeDtypeStruct((rows, cols), F32),...  70.1 us
    unnamed x1, local copies, waits for them, and re-layouts  2.26 us

profile of v2, /device:TPU:72, one launch (start us, length us, event | category | flops | bytes accessed | tf_op | source)
XLA Modules:
  0.0 72.4 jit_solution(16709045265110663085)
XLA Ops:
  0.0 70.1 %front.1 = f32[1024,256]{1,0:T(8,128)} custom-call(s32[2]{0:T(128)} %order_ref.1, f32[1024,256]{1,0:T(8,128)} %bitcast.1), custom_call_target="tpu_custom_call" | custom-call | tf_op jit(solution)/shard_map/front/pallas_call | solution.py:396
  70.1 2.3 %copy.4 = f32[1024,256]{1,0:T(8,128)} copy(f32[1024,256]{1,0:T(8,128)} %front.1) | data formatting | bytes 2097152

commit v3 on v2

--- a/solution.py
+++ b/solution.py
@@ -70,9 +70,9 @@
 
 
 def kernel(
-    order_ref, t_hbm, o_hbm,
-    t, f, u, ra, rb, rc, pa, pb, pc, za, zb, zc, xh, xa, dx, yb, xf, mat,
-    in_sem, out_sem, ssem, rsem,
+    order_hbm, t_hbm, u,
+    order_ref, t, f, ra, rb, rc, pa, pb, pc, za, zb, zc, xh, xa, dx, yb, xf, mat,
+    in_sem, ssem, rsem,
 ):
     layer, x, col = lax.axis_index("layer"), lax.axis_index("row"), lax.axis_index("col")
     y, zl, k = layer // 2, col // 2, lax.rem(col, 2)
@@ -118,6 +118,7 @@
             ]
         )
     ]
+    loads.append(pltpu.make_async_copy(order_hbm, order_ref, in_sem.at[3]))
     for c in loads:
         c.start()
 
@@ -162,18 +163,19 @@
     panel = x < 2
     plain, inner = jnp.logical_not(panel), jnp.logical_not(source)
     leaf = jnp.logical_not(source | relay)
-    pl.when(plain & inner)(zx[a].start)
+    far = (zl == 3) | (zl == 4) | (zl == 5)
+    near = jnp.logical_not(source | far)
+    pl.when(plain)(zx[a].start)
     half_sum(bs[0])
-    pl.when(panel & inner)(zx[a].start)
+    pl.when(panel)(zx[a].start)
     pl.when(plain)(zx[bs[0]].start)
     for c in bs[1:]:
         half_sum(c)
     pl.when(panel)(zx[bs[0]].start)
     for c in bs[1:]:
         zx[c].start()
-    pl.when(source)(zx[a].start)
     half_sum(cs[0])
-    pl.when(leaf)(zx[cs[0]].start)
+    pl.when(inner)(zx[cs[0]].start)
 
     slot = jnp.minimum(x, 2)
     rows_y = pl.ds(pl.multiple_of(y * 32, 8), 32)
@@ -258,7 +260,7 @@
         def _():
             copy(i, here, here, other).wait_recv()
 
-        if cond is relay:
+        if cond is near:
             start(copy(i, here, here, dev(y, z + 2, x, k), i), zl == 2)
             start(copy(i2, here, here, dev(y, z + 1, x, k), i), zl == 2)
             start(copy(i, here, here, dev(y, z - 1, x, k), i), zl == 6)
@@ -266,13 +268,14 @@
 
     for i, j in plane:
         pl.when(lax.rem(x - i + 4, 4) < 2)(across(i, j).wait_recv)
-    gather(bs[0])
-    pl.when(source)(zx[cs[0]].start)
     sib = copy(new(), dx.at[0:2, k], dx.at[0:2, k], other)
     start(sib)
     sib2 = copy(new(), dx.at[2, k], dx.at[2, k], other)
+    gather(bs[0])
+    pl.when(source)(zx[cs[0]].start)
     sib.wait_recv()
 
+    loads[3].wait()
     first = order_ref[0]
     swapped = jnp.full((NB, NB), first, jnp.int32) == 1
     d00, d01, d10, d11 = dx[0, 0], dx[0, 1], dx[1, 0], dx[1, 1]
@@ -280,8 +283,9 @@
     dpq, dqp = jnp.where(swapped, d10, d01), jnp.where(swapped, d01, d10)
 
     mat[0] = inverse_steps(dpp, 0, 8)
-    pass_on(bs[0], relay)
-    pl.when(relay)(zx[cs[0]].start)
+    pass_on(bs[0], near)
+    for c in cs[1:]:
+        pl.when(relay)(zx[c].start)
     for c in bs[1:]:
         gather(c)
     for c in cs[1:]:
@@ -293,11 +297,10 @@
     mat[1] = dqq - dot(dqp, w)
     mat[1] = inverse_steps(mat[1], 0, 8)
     for c in bs[1:]:
-        pass_on(c, relay)
-    for c in cs[1:]:
-        pl.when(relay)(zx[c].start)
+        pass_on(c, near)
     mat[1] = inverse_steps(mat[1], 8, 16)
     qinv = mat[1]
+    pass_on(bs[0], far)
     columns(plain)
 
     for d in (1, 2, 3):
@@ -348,44 +351,42 @@
     pl.when(plain)(sib2.wait_recv)
     x0 = jnp.concatenate([dx[slot, 0], dx[slot, 1]], 1)
     u[0:NB, :] = jnp.where(drop0, 0.0, f[0:NB, :]) - dot(x0, g0)
-    outs = []
-
-    def put(r, cols):
-        outs.append(pltpu.make_async_copy(u.at[r, cols], o_hbm.at[r, cols], out_sem.at[len(outs)]))
-        outs[-1].start()
-
-    put(slice(0, NB), slice(0, 256))
     side = {}
-    pass_on(bs[0], leaf)
-    gather(cs[-1])
-    for c in bs[1:]:
-        pass_on(c, leaf)
-    for c in bs:
+
+    def swap(c):
         for d in (1, 2, 3):
             xg[c, d].wait_recv()
         here = xf.at[k, :, c.sub]
         side[c] = copy(new(), here, here, other)
         start(side[c])
-    for c in bs:
+
+    def product(c):
         side[c].wait_recv()
-    for i in range(4):
-        u[NB + i * PART : NB + (i + 1) * PART, :] = dot(
-            jnp.concatenate([xf[0, i], xf[1, i]], 1), g
-        )
+        for i in range(4):
+            r = NB + i * PART + c.off
+            both = jnp.concatenate([xf[0, i, c.sub], xf[1, i, c.sub]], 1)
+            u[r : r + c.rows, :] = dot(both, g)
+
+    for c in bs[1:]:
+        pass_on(c, far)
+    swap(bs[0])
+    gather(cs[-1])
+    product(bs[0])
+    for c in bs[1:]:
+        swap(c)
+    for c in bs[1:]:
+        product(c)
     for c in chunks[1:]:
         for d in (1, 2, 3):
             ag[c, d].wait_recv()
         for i in range(4):
             r = slice(NB + i * PART + c.off, NB + i * PART + c.off + c.rows)
             u[r, c.cols] = f[r, c.cols] - u[r, c.cols]
-            put(r, c.cols)
     for c, cond in sends:
         if cond is None:
             c.wait_send()
         else:
             pl.when(cond)(c.wait_send)
-    for c in outs:
-        c.wait()
 
 
 def solution(mesh):
@@ -393,29 +394,33 @@
 
     def body(terms, order):
         vm = lambda *s: pltpu.VMEM(s, F32)
+        order, terms = (
+            pltpu.with_memory_space_constraint(v, pltpu.HBM)
+            for v in (order, terms.reshape(rows, cols))
+        )
         return pl.pallas_call(
             kernel,
             out_shape=jax.ShapeDtypeStruct((rows, cols), F32),
             in_specs=[
-                pl.BlockSpec(memory_space=pltpu.SMEM),
-                pl.BlockSpec(memory_space=pl.ANY),
+                pl.BlockSpec(memory_space=pltpu.HBM),
+                pl.BlockSpec(memory_space=pltpu.HBM),
             ],
-            out_specs=pl.BlockSpec(memory_space=pl.ANY),
+            out_specs=pl.BlockSpec(memory_space=pltpu.VMEM),
             scratch_shapes=[
-                vm(rows, cols), vm(rows, cols), vm(rows, cols),
+                pltpu.SMEM((2,), jnp.int32),
+                vm(rows, cols), vm(rows, cols),
                 vm(3, 32, 256), vm(3, PART, 128), vm(3, PART, 128),
                 vm(32, 256), vm(PART, 128), vm(PART, 128),
                 vm(32, 256), vm(PART, 128), vm(PART, 128),
                 vm(2, 32, 128), vm(32, 128), vm(3, 2, 128, 128), vm(2, 128, 256),
                 vm(2, 4, PART, 128), vm(2, 128, 128),
-                pltpu.SemaphoreType.DMA((3,)),
-                pltpu.SemaphoreType.DMA((1 + 8 * len(SPLIT),)),
+                pltpu.SemaphoreType.DMA((4,)),
                 pltpu.SemaphoreType.DMA((128,)),
                 pltpu.SemaphoreType.DMA((128,)),
             ],
-            compiler_params=pltpu.CompilerParams(collective_id=0, has_side_effects=True),
+            compiler_params=pltpu.CompilerParams(collective_id=0, has_side_effects=True, vmem_limit_bytes=48 << 20),
             name="front",
-        )(order, terms.reshape(rows, cols))
+        )(order, terms)
 
     return jax.shard_map(
         body,

time: 72.5 us -> 66.5 us (0.917)
  the two profiles are of different devices: /device:TPU:72 before, /device:TPU:103 now
where the time goes in v3:
time: 66.5 us; the launch traced here: 66.4 us
  Pallas kernels  65.4 us (98%)
  local copies, waits for them, and re-layouts  0.97 us (1%)
    pallas_call x1, Pallas kernels, body(): pl.pallas_call(kernel, out_shape=jax.ShapeDtypeStruct((rows, cols), F32),...  65.4 us

profile of v3, /device:TPU:103, one launch (start us, length us, event | category | flops | bytes accessed | tf_op | source)
XLA Modules:
  0.0 66.4 jit_solution(10371928409911855999)
XLA Ops:
  0.0 65.4 %front.1 = f32[1024,256]{1,0:T(8,128)S(1)} custom-call(s32[2]{0:T(128)} %order_hbm.1, f32[1024,256]{1,0:T(8,128)} %bitcast.1), custom_call_target="tpu_custom_call" | custom-call | tf_op jit(solution)/shard_map/front/pallas_call | solution.py:401
  65.4 1.0 %copy.4 = f32[1024,256]{1,0:T(8,128)} copy(f32[1024,256]{1,0:T(8,128)S(1)} %front.1) | data formatting | bytes 2097152

commit v4 on v3

--- a/solution.py
+++ b/solution.py
@@ -11,7 +11,7 @@
 NB = 128
 F32 = jnp.float32
 PART = 224
-SPLIT = (112, 112)
+SPLIT = (96, 128)
 
 
 def dev(y, z, x, k):

time: 66.5 us -> 66.3 us (level)
  the two profiles are of different devices: /device:TPU:103 before, /device:TPU:4 now
where the time goes in v4:
time: 66.3 us; the launch traced here: 66.2 us
  Pallas kernels  65.2 us (98%)
  local copies, waits for them, and re-layouts  0.97 us (1%)
    pallas_call x1, Pallas kernels, body(): pl.pallas_call(kernel, out_shape=jax.ShapeDtypeStruct((rows, cols), F32),...  65.2 us

profile of v4, /device:TPU:4, one launch (start us, length us, event | category | flops | bytes accessed | tf_op | source)
XLA Modules:
  0.0 66.2 jit_solution(5162312287260048875)
XLA Ops:
  0.0 65.2 %front.1 = f32[1024,256]{1,0:T(8,128)S(1)} custom-call(s32[2]{0:T(128)} %order_hbm.1, f32[1024,256]{1,0:T(8,128)} %bitcast.1), custom_call_target="tpu_custom_call" | custom-call | tf_op jit(solution)/shard_map/front/pallas_call | solution.py:401
  65.2 1.0 %copy.4 = f32[1024,256]{1,0:T(8,128)} copy(f32[1024,256]{1,0:T(8,128)S(1)} %front.1) | data formatting | bytes 2097152

commit v5 on v4

--- a/solution.py
+++ b/solution.py
@@ -11,7 +11,7 @@
 NB = 128
 F32 = jnp.float32
 PART = 224
-SPLIT = (96, 128)
+SPLIT = (88, 136)
 
 
 def dev(y, z, x, k):

time: 66.3 us -> 67.1 us (1.012)
  Pallas kernels: 65.2 us -> 66 us
    pallas_call x1, Pallas kernels: 65.2 us -> 66 us  [body(): pl.pallas_call(kernel, out_shape=jax.ShapeDtypeStruct((rows, cols), F32),...]
where the time goes in v5:
time: 67.1 us; the launch traced here: 67 us
  Pallas kernels  66 us (98%)
  local copies, waits for them, and re-layouts  0.97 us (1%)
    pallas_call x1, Pallas kernels, body(): pl.pallas_call(kernel, out_shape=jax.ShapeDtypeStruct((rows, cols), F32),...  66 us

profile of v5, /device:TPU:4, one launch (start us, length us, event | category | flops | bytes accessed | tf_op | source)
XLA Modules:
  0.0 67.0 jit_solution(9774778965097195417)
XLA Ops:
  0.0 66.0 %front.1 = f32[1024,256]{1,0:T(8,128)S(1)} custom-call(s32[2]{0:T(128)} %order_hbm.1, f32[1024,256]{1,0:T(8,128)} %bitcast.1), custom_call_target="tpu_custom_call" | custom-call | tf_op jit(solution)/shard_map/front/pallas_call | solution.py:401
  66.1 1.0 %copy.4 = f32[1024,256]{1,0:T(8,128)} copy(f32[1024,256]{1,0:T(8,128)S(1)} %front.1) | data formatting | bytes 2097152
